TPU v7x, 256 devices: a whole 4x4x8 slice. The times are simulated.
256 devices in a mesh: tp: 8 (over z), dp: 4 (over y), pp: 8 (over x, core).
Axes of the slice: x: 4, y: 4, z: 8, core: 2. Of those that a mesh axis runs over, the one named last changes fastest.
Arguments:
- master: float32 [50304, 1024], P('tp')
- exp_avg: float32 [50304, 1024], P('tp')
- exp_avg_sq: float32 [50304, 1024], P('tp')
- stage_ids: int32 [8, 24, 256], P('pp', 'dp')
- stage_acts: bfloat16 [8, 24, 256, 1024], P('pp', 'dp')
Outputs:
- output 1: float32 [50304, 1024], P('tp')
- output 2: float32 [50304, 1024], P('tp')
- output 3: float32 [50304, 1024], P('tp')
- output 4: bfloat16 [50304, 1024], P('tp')
All inputs are finite; a program needn't handle non-finite values.
Results may differ from a plain program's by a relative error of at most 0.001.
Values sent between devices are 32-bit elements.
A program may use at most 768 MiB of HBM per device.

v0:
```python
import jax
import jax.numpy as jnp
from jax import lax
from jax.sharding import PartitionSpec as P

LEARN_RATE = 0.003
BETA_ONE = 0.9
BETA_TWO = 0.95
ADAM_EPS = 1e-8
WEIGHT_DECAY = 0.1
CLIP_NORM = 1.0
OPT_STEP = 10


def stage_grad(master_blk, tok_ids, tok_acts, n_stage):
    stage_idx = lax.axis_index("pp")
    vocab_dev, model_dim = master_blk.shape
    tok_count = tok_ids.shape[1] * tok_ids.shape[2]
    tok_flat = tok_ids.reshape(tok_count)
    act_flat = tok_acts.reshape(tok_count, model_dim)
    row_ids = lax.axis_index("tp") * vocab_dev + lax.broadcasted_iota(jnp.int32, (1, vocab_dev), 1)
    hit_mask = tok_flat[:, None] == row_ids
    logits = jnp.einsum("td,vd->tv", act_flat, master_blk.astype(jnp.bfloat16), preferred_element_type=jnp.float32)
    row_max = lax.pmax(jnp.max(logits, axis=1), "tp")
    exp_logits = jnp.exp(logits - row_max[:, None])
    row_sum = lax.psum(jnp.sum(exp_logits, axis=1), "tp")
    prob_mat = exp_logits / row_sum[:, None]
    dlogits = (jnp.where(hit_mask, prob_mat - 1.0, prob_mat) / tok_count).astype(jnp.bfloat16)
    coeff_mat = jnp.where(stage_idx == 0, hit_mask.astype(jnp.bfloat16), dlogits)
    contrib = jnp.einsum("tv,td->vd", coeff_mat, act_flat, preferred_element_type=jnp.float32)
    active = jnp.logical_or(stage_idx == 0, stage_idx == n_stage - 1)
    return jnp.where(active, contrib, 0.0)


def adamw_update(master, exp_avg, exp_avg_sq, gradient):
    sq_total = lax.psum(jnp.sum(gradient * gradient), "tp")
    gradient = gradient * (CLIP_NORM / jnp.maximum(jnp.sqrt(sq_total), CLIP_NORM))
    new_avg = BETA_ONE * exp_avg + (1.0 - BETA_ONE) * gradient
    new_avg_sq = BETA_TWO * exp_avg_sq + (1.0 - BETA_TWO) * gradient * gradient
    step_dir = (new_avg / (1.0 - BETA_ONE ** OPT_STEP)) / (jnp.sqrt(new_avg_sq / (1.0 - BETA_TWO ** OPT_STEP)) + ADAM_EPS)
    new_master = master - LEARN_RATE * (step_dir + WEIGHT_DECAY * master)
    return new_master, new_avg, new_avg_sq, new_master.astype(jnp.bfloat16)


def solution(mesh):
    n_stage = mesh.shape["pp"]
    n_repl = mesh.shape["dp"]
    table_spec = P("tp", None)

    def device_step(master, exp_avg, exp_avg_sq, stage_ids, stage_acts):
        contrib = stage_grad(master, stage_ids, stage_acts, n_stage)
        stage_sum = lax.psum(contrib, "pp")
        gradient = lax.psum(stage_sum, "dp") / n_repl
        return adamw_update(master, exp_avg, exp_avg_sq, gradient)

    return jax.shard_map(device_step, mesh=mesh, in_specs=(table_spec, table_spec, table_spec, P("pp", "dp", None), P("pp", "dp", None, None)), out_specs=(table_spec, table_spec, table_spec, table_spec), check_vma=False)
```

profile of v0, /device:TPU:1, one launch (start us, length us, event | category | flops | bytes accessed | tf_op | source)
XLA Modules:
  0.0 944.1 jit_solution(3775775063737997088)
XLA Ops:
  7.2 0.0 copy-start
  7.2 0.0 all-reduce.3.cloned.1.call-start
  7.2 0.9 reduce
  8.1 0.9 copy-done
  9.1 30.5 %fusion.17 = (f32[1536]{0:T(1024)S(1)}, f32[1536,6288]{0,1:T(8,128)}) fusion(bf16[1536,1024]{1,0:T(8,128)(2,1)S(1)} %bitcast.3, f32[6288,1024]{1,0:T(8,128)} %param.5), kind=kOutput, calls=%fused_computation.21 | convolution fusion | flops 19796432896 | bytes 67540992 | tf_op jit(solution)/shard_map/td,vd->tv/dot_general | solution.py:23
  39.6 17.5 %pmax.7 = f32[1536]{0:T(1024)S(1)} all-reduce(f32[1536]{0:T(1024)S(1)} %get-tuple-element.8), channel_id=1, replica_groups=mesh['tp'=8,'dp'=4,'pp'=8] {'tp'}, use_global_device_ids=true, to_apply=%region_1.0 | all-reduce | flops 1536 | bytes 12288 | tf_op jit(solution)/shard_map/pmax | solution.py:24
  57.0 15.1 %fusion.2 = f32[1536]{0:T(1024)S(1)} fusion(f32[1536,6288]{0,1:T(8,128)} %get-tuple-element.9, f32[1536]{0:T(1024)S(1)} %pmax.7), kind=kLoop, calls=%fused_computation.6 | loop fusion | flops 19315200 | bytes 38645760 | tf_op jit(solution)/shard_map/reduce_sum | solution.py:26
  72.1 11.2 %psum.28 = f32[1536]{0:T(1024)S(1)} all-reduce(f32[1536]{0:T(1024)S(1)} %fusion.2), channel_id=1, replica_groups=mesh['tp'=8,'dp'=4,'pp'=8] {'tp'}, use_global_device_ids=true, to_apply=%region_3.0 | all-reduce | flops 1536 | bytes 12288 | tf_op jit(solution)/shard_map/psum | solution.py:26
  83.3 34.6 %fusion.8 = f32[6288,1024]{1,0:T(8,128)} fusion(bf16[1536,1024]{1,0:T(8,128)(2,1)S(1)} %bitcast.4, f32[1536,6288]{0,1:T(8,128)} %get-tuple-element.9, f32[1536]{0:T(1024)S(1)} %psum.28, f32[1536]{0:T(1024)S(1)} %pmax.7, s32[1536]{0:T(1024)S(1)} %eq.24, s32[6288]{0:T(1024)S(1)} %iota_add_fusion, pred[]{:T(512)S(6)} %eq.22, pred[]{:T(512)S(6)} %or.3), kind=kOutput, calls=%fused_computation.14 | convolution fusion | flops 19873701888 | bytes 67578432 | tf_op jit(solution)/shard_map/tv,td->vd/dot_general | solution.py:30
  117.9 0.0 all-reduce.3.cloned.1.call-update
  117.9 0.0 all-reduce.5.cloned.1.call-start
  118.0 278.2 %all-reduce.3.cloned.1.call-done = f32[6288,1024]{1,0:T(8,128)} async-done(((f32[6288,1024]{1,0:T(8,128)}), f32[6288,1024]{1,0:T(8,128)}) %all-reduce.3.cloned.1.call-update) | async-done | bytes 25755664 | tf_op jit(solution)/shard_map/psum | solution.py:52
  396.2 0.0 all-reduce.5.cloned.1.call-update
  396.2 447.4 %all-reduce.5.cloned.1.call-done = f32[6288,1024]{1,0:T(8,128)} async-done(((f32[6288,1024]{1,0:T(8,128)}), f32[6288,1024]{1,0:T(8,128)}) %all-reduce.5.cloned.1.call-update) | async-done | bytes 25755664 | tf_op jit(solution)/shard_map/psum | solution.py:53
  843.6 12.3 %multiply_reduce_fusion = f32[]{:T(128)} fusion(f32[6288,1024]{1,0:T(8,128)} %all-reduce.5.cloned.1.call-done), kind=kLoop, calls=%fused_computation.10 | loop fusion | flops 19316736 | bytes 25755652 | tf_op jit(solution)/shard_map/reduce_sum | solution.py:36
  856.0 14.5 %psum.31 = f32[]{:T(128)} all-reduce(f32[]{:T(128)} %multiply_reduce_fusion), channel_id=1, replica_groups=mesh['tp'=8,'dp'=4,'pp'=8] {'tp'}, use_global_device_ids=true, to_apply=%region_7.8 | all-reduce | flops 1 | bytes 8 | tf_op jit(solution)/shard_map/psum | solution.py:36
  871.2 0.0 copy-start.1
  871.2 66.0 %fusion.15 = (bf16[6288,1024]{1,0:T(8,128)(2,1)}, f32[6288,1024]{1,0:T(8,128)}, f32[6288,1024]{1,0:T(8,128)}, f32[6288,1024]{1,0:T(8,128)}) fusion(f32[6288,1024]{1,0:T(8,128)} %param.5, f32[6288,1024]{1,0:T(8,128)} %all-reduce.5.cloned.1.call-done, f32[]{:T(128)S(6)} %mul.51, f32[6288,1024]{1,0:T(8,128)} %param.6, f32[6288,1024]{1,0:T(8,128)} %param.7), kind=kLoop, calls=%fused_computation.20 | loop fusion | flops 109461504 | bytes 193167360 | tf_op jit(solution)/shard_map/convert_element_type | solution.py:42
  937.2 0.0 copy-done.1
  (2 shorter events, 0.0 us)
Async XLA Ops:
  7.2 1.9 copy-start
  7.2 389.0 %all-reduce.3.cloned.1.call-start = ((), (), s32[]{:S(2)}) async-start(), calls=%async_computation | async-start | bytes 51511296 | tf_op jit(solution)/shard_map/psum | solution.py:52
  117.9 725.7 %all-reduce.5.cloned.1.call-start = ((), (), s32[]{:S(2)}) async-start(), calls=%async_computation.1 | async-start | bytes 51511296 | tf_op jit(solution)/shard_map/psum | solution.py:53
  871.2 66.0 %copy-start.1 = (bf16[1,6,256,1024]{3,2,1,0:T(8,128)(2,1)S(1)}, bf16[1,6,256,1024]{3,2,1,0:T(8,128)(2,1)}, u32[]{:S(2)}) copy-start(bf16[1,6,256,1024]{3,2,1,0:T(8,128)(2,1)} %param.9) | copy-start | bytes 9437188
Sparse Core Ops, SparseCore 0:
  118.0 278.1 all-reduce.2
  398.7 444.8 all-reduce.4
where the time goes:
time: 948 us; the launch traced here: 944 us
  waiting for transfers between devices  726 us (77%)
  other arithmetic  94.2 us (10%)
  matrix products  65.1 us (7%)
  blocking collectives  43.2 us (5%)
  between operations  14.9 us (2%)
    psum x1, waiting for transfers between devices, device_step(): gradient = lax.psum(stage_sum, 'dp') / n_repl  447 us
    psum x1, waiting for transfers between devices, device_step(): stage_sum = lax.psum(contrib, 'pp')  278 us
    convert_element_type x1, other arithmetic, adamw_update(): return (new_master, new_avg, new_avg_sq, new_master.astype(jnp.bfloat16))  66 us
    dot_general x1, matrix products, stage_grad(): jnp.einsum('tv,td->vd', coeff_mat, act_flat, preferred_element_type=jnp.f...  34.6 us
    dot_general x1, matrix products, stage_grad(): jnp.einsum('td,vd->tv', act_flat, master_blk.astype(jnp.bfloat16), prefer...  30.5 us
  transfers between devices with their start and end apart: 2, of which 2 were waited for; matrix products, arithmetic and copies ran while one was open for 0% of the time, Pallas kernels for 0%

commit v1 on v0

v1 whole, which is shorter than its diff:
```python
import functools

import jax
import jax.numpy as jnp
from jax import lax
from jax.experimental import pallas as pl
from jax.experimental.pallas import tpu as pltpu
from jax.sharding import PartitionSpec as P

LEARN_RATE = 0.003
BETA_ONE = 0.9
BETA_TWO = 0.95
ADAM_EPS = 1e-8
WEIGHT_DECAY = 0.1
CLIP_NORM = 1.0
OPT_STEP = 10

MESH_ID = pl.DeviceIdType.MESH
LOW = -1e30


def stats_kernel(n_pp, n_tp, loc_ref, out_ref, buf_p, buf_z, mid, send_p, recv_p, send_z, recv_z):
    p = lax.axis_index("pp")
    z = lax.axis_index("tp")
    barrier = pltpu.get_barrier_semaphore()
    for o in range(1, n_pp):
        pl.semaphore_signal(barrier, inc=1, device_id={"pp": lax.rem(p + o, n_pp)}, device_id_type=MESH_ID)
    for o in range(1, n_tp):
        pl.semaphore_signal(barrier, inc=1, device_id={"tp": lax.rem(z + o, n_tp)}, device_id_type=MESH_ID)
    pl.semaphore_wait(barrier, n_pp + n_tp - 2)

    def exchange(src, buf, send, recv, axis, me, n):
        copies = []
        for o in range(1, n):
            copies.append(pltpu.make_async_remote_copy(
                src_ref=src, dst_ref=buf.at[o - 1], send_sem=send.at[o - 1], recv_sem=recv.at[o - 1],
                device_id={axis: lax.rem(me + o, n)}, device_id_type=MESH_ID))
        for c in copies:
            c.start()
        for c in copies:
            c.wait()
        top = src[0:1, :]
        for o in range(1, n):
            top = jnp.maximum(top, buf[o - 1, 0:1, :])
        tot = src[1:2, :] * jnp.exp(src[0:1, :] - top)
        for o in range(1, n):
            tot = tot + buf[o - 1, 1:2, :] * jnp.exp(buf[o - 1, 0:1, :] - top)
        return top, tot

    top, tot = exchange(loc_ref, buf_p, send_p, recv_p, "pp", p, n_pp)
    mid[0:1, :] = top
    mid[1:2, :] = tot
    top, tot = exchange(mid, buf_z, send_z, recv_z, "tp", z, n_tp)
    out_ref[0:1, :] = top
    out_ref[1:2, :] = tot


def merge_stats(stats, n_pp, n_tp):
    shape = stats.shape
    return pl.pallas_call(
        functools.partial(stats_kernel, n_pp, n_tp),
        out_shape=jax.ShapeDtypeStruct(shape, jnp.float32),
        in_specs=[pl.BlockSpec(memory_space=pltpu.VMEM)],
        out_specs=pl.BlockSpec(memory_space=pltpu.VMEM),
        scratch_shapes=[
            pltpu.VMEM((n_pp - 1, *shape), jnp.float32), pltpu.VMEM((n_tp - 1, *shape), jnp.float32),
            pltpu.VMEM(shape, jnp.float32),
            pltpu.SemaphoreType.DMA((n_pp - 1,)), pltpu.SemaphoreType.DMA((n_pp - 1,)),
            pltpu.SemaphoreType.DMA((n_tp - 1,)), pltpu.SemaphoreType.DMA((n_tp - 1,)),
        ],
        compiler_params=pltpu.CompilerParams(collective_id=0, has_side_effects=True),
        name="merge_stats",
    )(stats)


def cast_kernel(src_ref, out_ref):
    out_ref[...] = src_ref[...].astype(out_ref.dtype)


def to_bf16(arr):
    rows, dim = arr.shape
    spec = pl.BlockSpec((256, dim), lambda i: (i, 0))
    return pl.pallas_call(
        cast_kernel, out_shape=jax.ShapeDtypeStruct(arr.shape, jnp.bfloat16), grid=(rows // 256,),
        in_specs=[spec], out_specs=spec, name="to_bf16")(arr)


def adamw_kernel(scale_ref, e_ref, m_ref, v_ref, g_ref, *refs):
    ne_ref, nm_ref, nv_ref, nb_ref = refs[-4:]
    g = g_ref[...] * scale_ref[0, 0]
    e = e_ref[...]
    m = BETA_ONE * m_ref[...] + (1.0 - BETA_ONE) * g
    v = BETA_TWO * v_ref[...] + (1.0 - BETA_TWO) * g * g
    step = (m / (1.0 - BETA_ONE ** OPT_STEP)) / (jnp.sqrt(v / (1.0 - BETA_TWO ** OPT_STEP)) + ADAM_EPS)
    ne = e - LEARN_RATE * (step + WEIGHT_DECAY * e)
    ne_ref[...] = ne
    nm_ref[...] = m
    nv_ref[...] = v
    nb_ref[...] = ne.astype(jnp.bfloat16)


def adamw_chunk(scale, master, exp_avg, exp_avg_sq, grad, col, prev):
    rows, dim = master.shape
    width = grad.shape[1]
    tile = 256
    at = col // width
    wide = pl.BlockSpec((tile, width), lambda i: (i, at))
    narrow = pl.BlockSpec((tile, width), lambda i: (i, 0))
    f32 = jax.ShapeDtypeStruct((rows, dim), jnp.float32)
    bf16 = jax.ShapeDtypeStruct((rows, dim), jnp.bfloat16)
    extra = list(prev) if prev is not None else []
    count = rows * width
    return pl.pallas_call(
        adamw_kernel,
        out_shape=(f32, f32, f32, bf16),
        grid=(pl.cdiv(rows, tile),),
        in_specs=[pl.BlockSpec(memory_space=pltpu.SMEM), wide, wide, wide, narrow]
        + [pl.BlockSpec(memory_space=pl.ANY)] * len(extra),
        out_specs=(wide, wide, wide, wide),
        input_output_aliases={5 + i: i for i in range(len(extra))},
        cost_estimate=pl.CostEstimate(flops=20 * count, bytes_accessed=30 * count, transcendentals=2 * count),
        compiler_params=pltpu.CompilerParams(vmem_limit_bytes=58 << 20),
        name="adamw",
    )(scale, master, exp_avg, exp_avg_sq, grad, *extra)


def solution(mesh):
    n_pp, n_dp, n_tp = mesh.shape["pp"], mesh.shape["dp"], mesh.shape["tp"]
    table_spec = P("tp", None)

    def device_step(master, exp_avg, exp_avg_sq, stage_ids, stage_acts):
        vocab, dim = master.shape
        p, z = lax.axis_index("pp"), lax.axis_index("tp")
        tok = stage_ids.shape[1] * stage_ids.shape[2]
        n_blk = n_pp * n_dp
        rows = -(-vocab // n_blk)
        rows = -(-rows // 8) * 8
        part = tok // (n_tp * n_pp)

        acts = stage_acts.reshape(n_tp, n_pp, part, dim)
        mine = lax.dynamic_index_in_dim(acts, z, 0, keepdims=False).astype(jnp.float32)
        got = lax.all_to_all(mine, "pp", 0, 0, tiled=False)
        hid = lax.all_gather(got[n_pp - 1], ("tp", "pp"), tiled=True)
        dx = lax.all_gather(got[0], ("tp", "pp"), tiled=True)
        hid, dx = to_bf16(hid), to_bf16(dx)
        ids = stage_ids.reshape(1, 1, tok)
        ids = lax.all_gather(ids, "pp", axis=0, tiled=True)
        labels, lookup = ids[n_pp - 1], ids[0]

        blocks, index = [], []
        for d in range(n_dp):
            first = (d * n_pp + p) * rows
            short = max(0, ((d + 1) * n_pp) * rows - vocab)
            start = jnp.minimum(first, vocab - rows)
            blk = lax.dynamic_slice_in_dim(master, start, rows, 0).astype(jnp.bfloat16)
            if short:
                blk = jnp.concatenate([blk, jnp.zeros((short, dim), jnp.bfloat16)], 0)
                blk = lax.dynamic_slice_in_dim(blk, first - start, rows, 0)
            blocks.append(blk)
            index.append(first + lax.broadcasted_iota(jnp.int32, (rows, 1), 0))
        table = jnp.concatenate(blocks, 0)
        row_loc = jnp.concatenate(index, 0)
        valid = row_loc < vocab
        row_id = jnp.where(valid, row_loc + z * vocab, -1)

        logits = jnp.einsum("vd,td->vt", table, hid, preferred_element_type=jnp.float32)
        logits = jnp.where(valid, logits, LOW)
        top = jnp.max(logits, axis=0, keepdims=True)
        tot = jnp.sum(jnp.exp(logits - top), axis=0, keepdims=True)
        stats = merge_stats(jnp.concatenate([top, tot], 0), n_pp, n_tp)
        prob = jnp.exp(logits - stats[0:1]) / stats[1:2]
        hit = labels == row_id
        dlog = (jnp.where(hit, prob - 1.0, prob) / tok).astype(jnp.bfloat16)
        part_grad = jnp.einsum("vt,td->vd", dlog, hid, preferred_element_type=jnp.float32)
        look = (lookup == row_id).astype(jnp.bfloat16)
        part_grad = part_grad + jnp.einsum("vt,td->vd", look, dx, preferred_element_type=jnp.float32)

        grad = lax.psum_scatter(part_grad, "dp", scatter_dimension=0, tiled=True) / n_dp
        sq_total = lax.psum(jnp.sum(grad * grad), ("tp", "dp", "pp"))
        scale = (CLIP_NORM / jnp.maximum(jnp.sqrt(sq_total), CLIP_NORM)).reshape(1, 1)
        outs = None
        n_chunk = 2
        width = dim // n_chunk
        for k in range(n_chunk):
            full = lax.all_gather(grad[:, k * width:(k + 1) * width], ("dp", "pp"), tiled=True)
            outs = adamw_chunk(scale, master, exp_avg, exp_avg_sq, full, k * width, outs)
        return tuple(outs)

    return jax.shard_map(device_step, mesh=mesh, in_specs=(table_spec, table_spec, table_spec, P("pp", "dp", None), P("pp", "dp", None, None)), out_specs=(table_spec, table_spec, table_spec, table_spec), check_vma=False)
```

time: 948 us -> 462 us (0.49)
  waiting for transfers between devices: 726 us -> 198 us
  Pallas kernels: 0 us -> 111 us
  other arithmetic: 94.2 us -> 5.88 us
  blocking collectives: 43.2 us -> 108 us
  matrix products: 65.1 us -> 13.8 us
    psum x2 -> x0, waiting for transfers between devices: 726 us -> none  [the longest x1 447 us: device_step(): gradient = lax.psum(stage_sum, 'dp') / n_repl]
    all_gather x0 -> x4, waiting for transfers between devices: none -> 156 us  [the longest x1 74.5 us: device_step(): dx = lax.all_gather(got[0], ('tp', 'pp'), tiled=True)]
    pallas_call x0 -> x5, Pallas kernels: none -> 111 us  [the longest x2 87.1 us: adamw_chunk(): pl.pallas_call(adamw_kernel, out_shape=(f32, f32, f32, bf16), grid=(pl.cd...]
    convert_element_type x1, other arithmetic: 66 us -> 1.07 us  [device_step(): lax.dynamic_index_in_dim(acts, z, 0, keepdims=False).astype(jnp.float32)]
    dot_general x2 -> x3, matrix products: 65.1 us -> 13.8 us  [the longest x1 5.03 us: device_step(): jnp.einsum('vt,td->vd', dlog, hid, preferred_element_type=jnp.float32)]
    psum x2 -> x1, blocking collectives: 25.7 us -> 76.6 us  [device_step(): sq_total = lax.psum(jnp.sum(grad * grad), ('tp', 'dp', 'pp'))]
    reduce_scatter x0 -> x1, waiting for transfers between devices: none -> 40.2 us  [device_step(): lax.psum_scatter(part_grad, 'dp', scatter_dimension=0, tiled=True) / n_dp]
    reduce_sum x2 -> x1, other arithmetic: 27.4 us -> 0.89 us  [device_step(): tot = jnp.sum(jnp.exp(logits - top), axis=0, keepdims=True)]
  transfers between devices with their start and end apart: 2 -> 5, of which waited for: 2 -> 4; matrix products, arithmetic and copies ran while one was open for 0% -> 1% of each run, Pallas kernels for 0% -> 11%
where the time goes in v1:
time: 462 us; the launch traced here: 460 us
  waiting for transfers between devices  198 us (43%)
  Pallas kernels  111 us (24%)
  blocking collectives  108 us (23%)
  between operations  14.7 us (3%)
  matrix products  13.8 us (3%)
  local copies, waits for them, and re-layouts  8.69 us (2%)
  other arithmetic  5.88 us (1%)
    pallas_call x2, Pallas kernels, adamw_chunk(): pl.pallas_call(adamw_kernel, out_shape=(f32, f32, f32, bf16), grid=(pl.cd...  87.1 us
    psum x1, blocking collectives, device_step(): sq_total = lax.psum(jnp.sum(grad * grad), ('tp', 'dp', 'pp'))  76.6 us
    all_gather x1, waiting for transfers between devices, device_step(): dx = lax.all_gather(got[0], ('tp', 'pp'), tiled=True)  74.5 us
    all_gather x1, waiting for transfers between devices, device_step(): hid = lax.all_gather(got[n_pp - 1], ('tp', 'pp'), tiled=True)  62.8 us
    reduce_scatter x1, waiting for transfers between devices, device_step(): lax.psum_scatter(part_grad, 'dp', scatter_dimension=0, tiled=True) / n_dp  40.2 us
    all_gather x2, waiting for transfers between devices, device_step(): lax.all_gather(grad[:, k * width:(k + 1) * width], ('dp', 'pp'), tiled=True)  18.8 us
    all_to_all x1, blocking collectives, device_step(): got = lax.all_to_all(mine, 'pp', 0, 0, tiled=False)  17.7 us
    all_gather x1, blocking collectives, device_step(): ids = lax.all_gather(ids, 'pp', axis=0, tiled=True)  13.7 us
  transfers between devices with their start and end apart: 5, of which 4 were waited for; matrix products, arithmetic and copies ran while one was open for 1% of the time, Pallas kernels for 11%

profile of v1, /device:TPU:1, one launch (start us, length us, event | category | flops | bytes accessed | tf_op | source)
XLA Modules:
  0.0 460.1 jit_solution(8631887630408811274)
XLA Ops:
  7.2 1.1 bitcast_convert_fusion
  8.3 17.7 %all_to_all.5 = f32[8,24,1024]{2,1,0:T(8,128)S(1)} all-to-all(f32[8,24,1024]{2,1,0:T(8,128)S(1)} %bitcast_convert_fusion), channel_id=1, replica_groups=mesh['tp'=8,'dp'=4,'pp'=8] {'pp'}, dimensions={0} | all-to-all | bytes 1572864 | tf_op jit(solution)/shard_map/all_to_all | solution.py:142
  26.0 0.7 fusion.27
  26.8 0.7 all-gather.13.cloned.1.call-update
  27.5 13.7 %all_gather.15 = s32[8,1,1536]{2,1,0:T(1,128)S(1)} all-gather(s32[1,1,1536]{2,1,0:T(1,128)} %bitcast.14), channel_id=1, replica_groups=mesh['tp'=8,'dp'=4,'pp'=8] {'pp'}, dimensions={0}, use_global_device_ids=true | all-gather | bytes 55296 | tf_op jit(solution)/shard_map/all_gather | solution.py:147
  43.2 3.2 dynamic-slice_convert_fusion.3
  46.6 62.8 %all-gather.11.cloned.1.call-done = f32[1,1536,1024]{2,1,0:T(8,128)} async-done(((f32[1,24,1024]{2,1,0:T(8,128)}), f32[1,1536,1024]{2,1,0:T(8,128)}) %all-gather.11.cloned.1.call-update) | async-done | bytes 6291472 | tf_op jit(solution)/shard_map/all_gather | solution.py:143
  109.3 5.9 %to_bf16.2 = bf16[1536,1024]{1,0:T(8,128)(2,1)} custom-call(f32[1536,1024]{1,0:T(8,128)} %bitcast.11), custom_call_target="tpu_custom_call" | custom-call | tf_op jit(solution)/shard_map/to_bf16/pallas_call | solution.py:83
  115.3 74.5 %all-gather.13.cloned.1.call-done = f32[1,1536,1024]{2,1,0:T(8,128)} async-done(((f32[1,24,1024]{2,1,0:T(8,128)}), f32[1,1536,1024]{2,1,0:T(8,128)}) %all-gather.13.cloned.1.call-update) | async-done | bytes 6291472 | tf_op jit(solution)/shard_map/all_gather | solution.py:144
  189.8 5.9 %to_bf16.3 = bf16[1536,1024]{1,0:T(8,128)(2,1)} custom-call(f32[1536,1024]{1,0:T(8,128)} %bitcast.12), custom_call_target="tpu_custom_call" | custom-call | tf_op jit(solution)/shard_map/to_bf16/pallas_call | solution.py:83
  195.8 4.0 select_reduce_fusion
  199.8 2.2 copy-done
  202.0 0.9 exponential_reduce_fusion
  203.6 12.1 %merge_stats.1 = f32[2,1536]{1,0:T(2,128)} custom-call(f32[2,1536]{1,0:T(2,128)} %pad_maximum_fusion.loc_ref), custom_call_target="tpu_custom_call" | custom-call | tf_op jit(solution)/shard_map/merge_stats/pallas_call | solution.py:60
  215.7 0.8 slice_reduce_fusion.3
  216.6 4.8 %fusion.2 = f32[800,1024]{1,0:T(8,128)S(1)} fusion(bf16[1536,1024]{1,0:T(8,128)(2,1)} %to_bf16.3, s32[1536]{0:T(1024)S(1)} %copy-done.4, s32[800]{0:T(1024)S(1)} %copy-done.5), kind=kOutput, calls=%fused_computation.4 | convolution fusion | flops 2517811200 | bytes 6431872 | tf_op jit(solution)/shard_map/vt,td->vd/dot_general | solution.py:176
  221.4 5.0 %fusion.10 = f32[800,1024]{1,0:T(8,128)} fusion(f32[800,1024]{1,0:T(8,128)S(1)} %fusion.2, bf16[1536,1024]{1,0:T(8,128)(2,1)S(1)} %copy-done.2, f32[800,1536]{1,0:T(8,128)S(1)} %copy-done.1, f32[1536]{0:T(1024)S(1)} %get-tuple-element.15, f32[1536]{0:T(1024)S(1)} %get-tuple-element.14, s32[1536]{0:T(1024)S(1)} %copy-done.3, s32[800]{0:T(1024)S(1)} %copy-done.5, ...), kind=kOutput, calls=%fused_computation.12 | convolution fusion | flops 2527232000 | bytes 14636960 | tf_op jit(solution)/shard_map/vt,td->vd/dot_general | solution.py:174
  226.5 40.2 %reduce-scatter.2.cloned.1.call-done = f32[200,1024]{1,0:T(8,128)} async-done(((f32[800,1024]{1,0:T(8,128)}), f32[200,1024]{1,0:T(8,128)}) %reduce-scatter.2.cloned.1.call-update) | async-done | bytes 819216 | tf_op jit(solution)/shard_map/reduce_scatter | solution.py:178
  266.7 2.0 broadcast_multiply_fusion
  268.7 1.0 fusion.26
  270.3 76.6 %psum.7 = f32[]{:T(128)} all-reduce(f32[]{:T(128)} %get-tuple-element.23), channel_id=1, replica_groups=mesh['tp'=8,'dp'=4,'pp'=8] {'tp','dp','pp'}, use_global_device_ids=true, to_apply=%region_4.5 | all-reduce | flops 1 | bytes 8 | tf_op jit(solution)/shard_map/psum | solution.py:179
  347.7 43.6 %adamw.2 = (f32[6288,1024]{1,0:T(8,128)}, f32[6288,1024]{1,0:T(8,128)}, f32[6288,1024]{1,0:T(8,128)}, bf16[6288,1024]{1,0:T(8,128)(2,1)}) custom-call(f32[1,1]{1,0:T(1,128)} %bitcast.5.scale_ref, f32[6288,1024]{1,0:T(8,128)} %e_ref.3, f32[6288,1024]{1,0:T(8,128)} %m_ref.3, f32[6288,1024]{1,0:T(8,128)} %v_ref.3, f32[6400,512]{1,0:T(8,128)} %all-gather.9.cloned.1.call-done.g_ref), custom_call_target="tpu_custom_call" | custom-call | flops 64389120 | bytes 96583680 | tf_op jit(solution)/shard_map/adamw/pallas_call | solution.py:113
  391.2 18.8 %all-gather.7.cloned.1.call-done.g_ref = f32[6400,512]{1,0:T(8,128)} async-done(((f32[200,512]{1,0:T(8,128)}), f32[6400,512]{1,0:T(8,128)}) %all-gather.7.cloned.1.call-update) | async-done | bytes 13107216 | tf_op jit(solution)/shard_map/all_gather | solution.py:185
  410.0 43.5 %adamw.3 = (f32[6288,1024]{1,0:T(8,128)}, f32[6288,1024]{1,0:T(8,128)}, f32[6288,1024]{1,0:T(8,128)}, bf16[6288,1024]{1,0:T(8,128)(2,1)}) custom-call(f32[1,1]{1,0:T(1,128)} %bitcast.5.scale_ref, f32[6288,1024]{1,0:T(8,128)} %e_ref.3, f32[6288,1024]{1,0:T(8,128)} %m_ref.3, ...), custom_call_target="tpu_custom_call", output_to_operand_aliasing={{0}: (5, {}), {1}: (6, {}), {2}: (7, {}), {3}: (8, {})} | custom-call | flops 64389120 | bytes 96583680 | tf_op jit(solution)/shard_map/adamw/pallas_call | solution.py:113
  (34 shorter events, 3.5 us)
Async XLA Ops:
  7.2 102.2 %all-gather.11.cloned.1.call-start = ((), (), s32[]{:S(2)}) async-start(), calls=%async_computation.5 | async-start | bytes 6389760 | tf_op jit(solution)/shard_map/all_gather | solution.py:143
  26.7 163.1 %all-gather.13.cloned.1.call-start = ((), (), s32[]{:S(2)}) async-start(), calls=%async_computation.6 | async-start | bytes 6389760 | tf_op jit(solution)/shard_map/all_gather | solution.py:144
  27.5 239.3 %reduce-scatter.2.cloned.1.call-start = ((), (), s32[]{:S(2)}) async-start(), calls=%async_computation.2 | async-start | bytes 4096000 | tf_op jit(solution)/shard_map/reduce_scatter | solution.py:178
  115.3 80.5 %copy-start.2 = (bf16[1536,1024]{1,0:T(8,128)(2,1)S(1)}, bf16[1536,1024]{1,0:T(8,128)(2,1)}, u32[]{:S(2)}) copy-start(bf16[1536,1024]{1,0:T(8,128)(2,1)} %to_bf16.2) | copy-start | bytes 9437188
  195.8 6.3 %copy-start.6 = (pred[800]{0:T(1024)(128)(4,1)S(1)}, pred[800]{0:T(1024)(128)(4,1)}, u32[]{:S(2)}) copy-start(pred[800]{0:T(1024)(128)(4,1)} %fusion.21) | copy-start | bytes 2404
  199.8 2.3 copy-start
  199.8 16.7 %copy-start.4 = (s32[1536]{0:T(1024)S(1)}, s32[1536]{0:T(1024)}, u32[]{:S(2)}) copy-start(s32[1536]{0:T(1024)} %get-tuple-element.13) | copy-start | bytes 18436
  199.8 16.7 %copy-start.5 = (s32[800]{0:T(1024)S(1)}, s32[800]{0:T(1024)}, u32[]{:S(2)}) copy-start(s32[800]{0:T(1024)} %add_select_fusion.1) | copy-start | bytes 9604
  216.5 4.8 %copy-start.1 = (f32[800,1536]{1,0:T(8,128)S(1)}, f32[800,1536]{1,0:T(8,128)}, u32[]{:S(2)}) copy-start(f32[800,1536]{1,0:T(8,128)} %copy-done) | copy-start | bytes 14745604
  216.6 4.8 %copy-start.3 = (s32[1536]{0:T(1024)S(1)}, s32[1536]{0:T(1024)}, u32[]{:S(2)}) copy-start(s32[1536]{0:T(1024)} %get-tuple-element.12) | copy-start | bytes 18436
  216.6 4.8 %copy-start.7 = (pred[800]{0:T(1024)(128)(4,1)S(1)}, pred[800]{0:T(1024)(128)(4,1)}, u32[]{:S(2)}) copy-start(pred[800]{0:T(1024)(128)(4,1)} %fusion.21) | copy-start | bytes 2404
  226.4 121.2 %all-gather.9.cloned.1.call-start = ((), (), s32[]{:S(2)}) async-start(), calls=%async_computation.4 | async-start | bytes 13516800 | tf_op jit(solution)/shard_map/all_gather | solution.py:185
  269.7 140.3 %all-gather.7.cloned.1.call-start = ((), (), s32[]{:S(2)}) async-start(), calls=%async_computation.3 | async-start | bytes 13516800 | tf_op jit(solution)/shard_map/all_gather | solution.py:185
Sparse Core Ops, SparseCore 0:
  26.8 82.4 all-gather.10
  112.7 77.1 all-gather.12
  226.6 40.1 reduce-scatter.1
  269.8 69.2 all-gather.8
  341.5 68.4 all-gather.6

commit v2 on v0

v2 whole, which is shorter than its diff:
```python
import functools

import jax
import jax.numpy as jnp
from jax import lax
from jax.experimental import pallas as pl
from jax.experimental.pallas import tpu as pltpu
from jax.sharding import PartitionSpec as P

LEARN_RATE = 0.003
BETA_ONE = 0.9
BETA_TWO = 0.95
ADAM_EPS = 1e-8
WEIGHT_DECAY = 0.1
CLIP_NORM = 1.0
OPT_STEP = 10

MESH_ID = pl.DeviceIdType.MESH
LOW = -1e30
VMEM = pltpu.VMEM
DMA = pltpu.SemaphoreType.DMA
F32, BF16 = jnp.float32, jnp.bfloat16


def remote(src, dst, send, recv, where):
    return pltpu.make_async_remote_copy(src_ref=src, dst_ref=dst, send_sem=send, recv_sem=recv, device_id=where, device_id_type=MESH_ID)


def in_vmem(arr):
    return pltpu.with_memory_space_constraint(arr, VMEM)


def enter(groups):
    barrier = pltpu.get_barrier_semaphore()
    for axis, peer in groups:
        pl.semaphore_signal(barrier, inc=1, device_id={axis: peer}, device_id_type=MESH_ID)
    pl.semaphore_wait(barrier, len(groups))


def spread_kernel(n_tp, n_pp, n_chunk, acts_ref, ids_ref, hid_ref, dx_ref, lab_ref, look_ref, hid_buf, dx_buf, feed_sem, send_x, send_z, send_d, send_e, recv_x, recv_z, recv_d, recv_e, id_send, id_recv):
    p, z = lax.axis_index("pp"), lax.axis_index("tp")
    n_x = n_pp // 2
    x, c, par = p // 2, lax.rem(p, 2), lax.rem(z, 2)
    step = 1 - 2 * c
    next_p = 2 * lax.rem(x + step + n_x, n_x) + c
    next_z = lax.rem(z + step + n_tp, n_tp)
    mate = 2 * x + 1 - c
    tok = hid_buf.shape[0]
    quarter = tok // 4
    size = quarter // n_chunk
    lag = 2

    enter([("pp", lax.rem(p + o, n_pp)) for o in range(1, n_pp)] + [("tp", lax.rem(z + 1, n_tp)), ("tp", lax.rem(z + n_tp - 1, n_tp))])

    def rows(core, parity, k):
        return pl.ds(pl.multiple_of((2 * parity + core) * quarter + k * size, 8), size)

    for a, source in enumerate((n_pp - 1, 0)):
        dst = (lab_ref, look_ref)[a]

        @pl.when(p == source)
        def _(a=a, dst=dst):
            dst[...] = ids_ref[...]
            for o in range(1, n_pp):
                remote(ids_ref, dst, id_send.at[a, o - 1], id_recv.at[a], {"pp": lax.rem(p + o, n_pp)}).start()

    for a, (source, buf, out) in enumerate(((n_pp - 1, hid_buf, hid_ref), (0, dx_buf, dx_ref))):
        s_x, s_c = source // 2, source % 2
        ahead = jnp.where(c == 0, x - s_x, s_x - x)
        dist = lax.rem(ahead + n_x, n_x)
        is_src = p == source

        def feed(k):
            there = rows(1 - c, par, k)
            return remote(acts_ref.at[there], buf.at[there], feed_sem.at[a, k], recv_x.at[a, k], {"pp": mate})

        def ring(k, src=buf):
            here = rows(c, par, k)
            return remote(src.at[here], buf.at[here], send_x.at[a, k], recv_x.at[a, k], {"pp": next_p})

        def plane(k, src=buf):
            here = rows(c, par, k)
            return remote(src.at[here], buf.at[here], send_z.at[a, k], recv_z.at[a, k], {"tp": next_z})

        def plane_in(k):
            here = rows(c, 1 - par, k)
            return remote(buf.at[here], buf.at[here], send_z.at[a, k], recv_z.at[a, k], {"tp": next_z})

        def across(k, src=buf):
            here = rows(c, par, k)
            return remote(src.at[here], buf.at[here], send_d.at[a, k], recv_d.at[a, k], {"pp": mate})

        def across_in(k):
            here = rows(1 - c, par, k)
            return remote(buf.at[here], buf.at[here], send_d.at[a, k], recv_d.at[a, k], {"pp": mate})

        def again(k):
            here = rows(c, 1 - par, k)
            return remote(buf.at[here], buf.at[here], send_e.at[a, k], recv_e.at[a, k], {"pp": mate})

        def again_in(k):
            here = rows(1 - c, 1 - par, k)
            return remote(buf.at[here], buf.at[here], send_e.at[a, k], recv_e.at[a, k], {"pp": mate})

        @pl.when(is_src)
        def _():
            @pl.loop(0, n_chunk)
            def _(k):
                feed(k).start()

        @pl.loop(0, n_chunk + lag)
        def _(k):
            @pl.when(k < n_chunk)
            def _():
                def onward(src):
                    if n_x > 1:
                        @pl.when(dist < n_x - 1)
                        def _():
                            ring(k, src).start()

                    plane(k, src).start()
                    across(k, src).start()

                @pl.when(is_src)
                def _():
                    onward(acts_ref)
                    here = rows(c, par, k)
                    buf[here, :] = acts_ref[here, :]

                @pl.when(jnp.logical_not(is_src))
                def _():
                    ring(k).wait_recv()
                    onward(buf)

            @pl.when(k >= lag)
            def _():
                plane_in(k - lag).wait_recv()
                again(k - lag).start()

        @pl.loop(0, n_chunk)
        def _(k):
            across_in(k).wait_recv()
            again_in(k).wait_recv()

        @pl.loop(0, tok // 128)
        def _(k):
            here = pl.ds(pl.multiple_of(k * 128, 128), 128)
            out[here, :] = buf[here, :].astype(BF16)

        @pl.loop(0, n_chunk)
        def _(k):
            @pl.when(is_src)
            def _():
                feed(k).wait_send()

            if n_x > 1:
                @pl.when(dist < n_x - 1)
                def _():
                    ring(k).wait_send()

            plane(k).wait_send()
            across(k).wait_send()
            again(k).wait_send()

    for a, source in enumerate((n_pp - 1, 0)):
        dst = (lab_ref, look_ref)[a]

        @pl.when(p == source)
        def _(a=a, dst=dst):
            for o in range(1, n_pp):
                remote(ids_ref, dst, id_send.at[a, o - 1], id_recv.at[a], {"pp": lax.rem(p + o, n_pp)}).wait_send()

        @pl.when(p != source)
        def _(a=a, dst=dst):
            remote(ids_ref, dst, id_send.at[a, 0], id_recv.at[a], {"pp": mate}).wait_recv()


def spread(acts, ids, n_tp, n_pp):
    tok, dim = acts.shape
    n_chunk = 12 if tok % (4 * 12 * 8) == 0 else 2
    sem = DMA((2, n_chunk))
    full = pl.BlockSpec(memory_space=VMEM)
    return pl.pallas_call(
        functools.partial(spread_kernel, n_tp, n_pp, n_chunk),
        out_shape=(VMEM((tok, dim), BF16), VMEM((tok, dim), BF16), jax.ShapeDtypeStruct(ids.shape, jnp.int32), jax.ShapeDtypeStruct(ids.shape, jnp.int32)),
        in_specs=[full, full],
        out_specs=(full, full, full, full),
        scratch_shapes=[VMEM((tok, dim), F32), VMEM((tok, dim), F32)] + [sem] * 9 + [DMA((2, n_pp - 1)), DMA((2,))],
        compiler_params=pltpu.CompilerParams(collective_id=0, has_side_effects=True, vmem_limit_bytes=32 << 20),
        name="spread",
    )(in_vmem(acts), ids)


def ring_plan(n_one, n_two):
    items = [(1, s, 0) for s in range(n_one - 1)] + [(2, s, t) for s in range(n_one) for t in range(n_two - 1)]
    return sorted(items, key=lambda i: (i[1] + i[2], i[0], i[2]))


def grad_kernel(n_tp, n_dp, n_pp, vocab, tab_ref, hid_ref, dx_ref, lab_ref, look_ref, g_ref, scale_ref, exp_ref, dl_ref, part_ref, stat_ref, mid_ref, buf_p, buf_z, rel_ref, one_ref, com_ref, nb_p, nb_y, nb_z, sp_s, sp_r, sz_s, sz_r, rs_s, rs_r, np_s, np_r, ny_s, ny_r, nz_s, nz_r, ag_s, ag_r, d_s, d_r):
    p, z, y = lax.axis_index("pp"), lax.axis_index("tp"), lax.axis_index("dp")
    n_x = n_pp // 2
    x, c = p // 2, lax.rem(p, 2)
    mate = 2 * x + 1 - c
    rows, tok = exp_ref.shape[1:]
    dq = g_ref.shape[3]
    up_y, down_y = lax.rem(y + 1, n_dp), lax.rem(y + n_dp - 1, n_dp)

    enter([("pp", lax.rem(p + o, n_pp)) for o in range(1, n_pp)] + [("tp", lax.rem(z + o, n_tp)) for o in range(1, n_tp)] + [("dp", lax.rem(y + o, n_dp)) for o in range(1, n_dp)])

    def first_row(d):
        return (d * n_pp + p) * rows

    wide = min(256, tok)

    @pl.loop(0, tok // wide)
    def _(j):
        cols = pl.ds(pl.multiple_of(j * wide, wide), wide)
        h = hid_ref[cols, :]
        top = jnp.full((1, wide), LOW, F32)
        for d in range(n_dp):
            lg = lax.dot_general(tab_ref[d], h, (((1,), (1,)), ((), ())), preferred_element_type=F32)
            if (d + 1) * n_pp * rows > vocab:
                ok = first_row(d) + lax.broadcasted_iota(jnp.int32, (rows, wide), 0) < vocab
                lg = jnp.where(ok, lg, LOW)
            exp_ref[d, :, cols] = lg
            top = jnp.maximum(top, jnp.max(lg, axis=0, keepdims=True))
        tot = jnp.zeros((1, wide), F32)
        for d in range(n_dp):
            e = jnp.exp(exp_ref[d, :, cols] - top)
            exp_ref[d, :, cols] = e
            tot = tot + jnp.sum(e, axis=0, keepdims=True)
        stat_ref[0:1, cols] = top
        stat_ref[1:2, cols] = tot

    def swap(src, buf, send, recv, axis, me, n):
        return [remote(src, buf.at[o - 1], send.at[o - 1], recv.at[o - 1], {axis: lax.rem(me + o, n)}) for o in range(1, n)]

    def merge(src, buf, n):
        top = src[0:1, :]
        for o in range(1, n):
            top = jnp.maximum(top, buf[o - 1, 0:1, :])
        tot = src[1:2, :] * jnp.exp(src[0:1, :] - top)
        for o in range(1, n):
            tot = tot + buf[o - 1, 1:2, :] * jnp.exp(buf[o - 1, 0:1, :] - top)
        return top, tot

    def local_ids(ref):
        ids = ref[...] - z * vocab
        return jnp.where(ids < vocab, ids, -1)

    def row_ids(d):
        return first_row(d) + lax.broadcasted_iota(jnp.int32, (rows, tok), 0)

    def lookup(d):
        dl_ref[...] = (local_ids(look_ref) == row_ids(d)).astype(BF16)
        for q in range(4):
            part_ref[d, q] = jnp.dot(dl_ref[...], dx_ref[:, q * dq:(q + 1) * dq], preferred_element_type=F32)

    stage = swap(stat_ref, buf_p, sp_s, sp_r, "pp", p, n_pp)
    for cp in stage:
        cp.start()
    pl.loop(0, n_dp // 2)(lookup)
    for cp in stage:
        cp.wait()
    top, tot = merge(stat_ref, buf_p, n_pp)
    mid_ref[0:1, :] = top
    mid_ref[1:2, :] = tot
    stage = swap(mid_ref, buf_z, sz_s, sz_r, "tp", z, n_tp)
    for cp in stage:
        cp.start()
    pl.loop(n_dp // 2, n_dp)(lookup)
    for cp in stage:
        cp.wait()
    top, tot = merge(mid_ref, buf_z, n_tp)
    mid_ref[0:1, :] = jnp.exp(stat_ref[0:1, :] - top) / (tot * tok)

    def head(d):
        prob = exp_ref[d] * mid_ref[0:1, :]
        hit = local_ids(lab_ref) == row_ids(d)
        dl_ref[...] = jnp.where(hit, prob - 1.0 / tok, prob).astype(BF16)
        for q in range(4):
            part_ref[d, q] += jnp.dot(dl_ref[...], hid_ref[:, q * dq:(q + 1) * dq], preferred_element_type=F32)

    lo, hi = pl.ds(0, 2), pl.ds(2, 2)
    far = lax.rem(y + 2, n_dp)
    rel_a = remote(part_ref.at[far, lo], rel_ref.at[0], rs_s.at[0], rs_r.at[0], {"dp": up_y})
    rel_b = remote(part_ref.at[far, hi], rel_ref.at[1], rs_s.at[1], rs_r.at[1], {"dp": down_y})
    one_b = remote(part_ref.at[up_y, hi], one_ref.at[1], rs_s.at[2], rs_r.at[2], {"dp": up_y})
    one_a = remote(part_ref.at[down_y, lo], one_ref.at[0], rs_s.at[3], rs_r.at[3], {"dp": down_y})
    com_a = remote(part_ref.at[up_y, lo], com_ref.at[0], rs_s.at[4], rs_r.at[4], {"dp": up_y})
    com_b = remote(part_ref.at[down_y, hi], com_ref.at[1], rs_s.at[5], rs_r.at[5], {"dp": down_y})
    head(far)
    rel_a.start()
    rel_b.start()
    head(up_y)
    one_b.start()
    head(down_y)
    one_a.start()
    head(y)
    rel_a.wait_recv()
    part_ref[up_y, lo] += rel_ref[0]
    com_a.start()
    rel_b.wait_recv()
    part_ref[down_y, hi] += rel_ref[1]
    com_b.start()
    own = y * n_pp + p
    square = jnp.zeros((8, 128), F32)
    one_a.wait_recv()
    one_b.wait_recv()
    for half, cp in ((0, com_a), (1, com_b)):
        cp.wait_recv()
        for q in range(2):
            total = (part_ref[y, 2 * half + q] + com_ref[half, q] + one_ref[half, q]) * (1.0 / n_dp)
            g_ref[own, 2 * half + q] = total
            lanes = jnp.sum((total * total).reshape(rows // 8, 8, dq), axis=0)
            for i in range(0, dq, 128):
                square = square + lanes[:, i:i + 128]

    def block(xx, yy):
        return lax.rem(yy + 2 * n_dp, n_dp) * n_pp + 2 * lax.rem(xx + 2 * n_x, n_x) + c

    colours = []
    for q, (axes, sign) in enumerate((("xy", 1), ("xy", -1), ("yx", 1), ("yx", -1))):
        sizes = (n_x, n_dp) if axes == "xy" else (n_dp, n_x)
        to_x = {"pp": 2 * lax.rem(x + sign + n_x, n_x) + c}
        to_y = {"dp": lax.rem(y + sign + n_dp, n_dp)}
        dest = (to_x, to_y) if axes == "xy" else (to_y, to_x)
        colours.append((q, axes, sign, sizes, dest, ring_plan(*sizes)))

    def holder(axes, sign, s, t):
        return block(x - sign * s, y - sign * t) if axes == "xy" else block(x - sign * t, y - sign * s)

    def message(colour, item, coming):
        q, axes, sign, _, dest, plan = colour
        phase, s, t = item
        at = plan.index(item)
        s_at, t_at = (s + coming, t) if phase == 1 else (s, t + coming)
        b = holder(axes, sign, s_at, t_at)
        return remote(g_ref.at[b, q], g_ref.at[b, q], ag_s.at[q, at], ag_r.at[q, at], dest[phase - 1])

    def mate_copy(q, slot, b):
        return remote(g_ref.at[b, q], g_ref.at[b, q], d_s.at[q, slot], d_r.at[q, slot], {"pp": mate})

    sends = []

    def push(cp):
        cp.start()
        sends.append(cp)

    for colour in colours:
        if colour[3][0] > 1:
            push(message(colour, (1, 0, 0), 0))
    for colour in colours:
        if colour[3][1] > 1:
            push(message(colour, (2, 0, 0), 0))

    def norm_swap(value, buf, send, recv, axis, me, n):
        buf[me] = value
        return [remote(buf.at[me], buf.at[me], send.at[o - 1], recv.at[o - 1], {axis: lax.rem(me + o, n)}) for o in range(1, n)], [
            remote(buf.at[lax.rem(me + n - o, n)], buf.at[lax.rem(me + n - o, n)], send.at[o - 1], recv.at[o - 1], {axis: lax.rem(me + o, n)}) for o in range(1, n)]

    norm_out, norm_in = norm_swap(square, nb_p, np_s, np_r, "pp", p, n_pp)
    for cp in norm_out:
        push(cp)
    for q in range(4):
        push(mate_copy(q, 0, own))

    steps = n_x * n_dp - 1
    for i in range(steps):
        for colour in colours:
            q, axes, sign, sizes, dest, plan = colour
            phase, s, t = plan[i]
            message(colour, plan[i], 1).wait_recv()
            if phase == 1:
                if s + 1 < sizes[0] - 1:
                    push(message(colour, (1, s + 1, 0), 0))
                if sizes[1] > 1:
                    push(message(colour, (2, s + 1, 0), 0))
                push(mate_copy(q, i + 1, holder(axes, sign, s + 1, 0)))
            else:
                if t + 1 < sizes[1] - 1:
                    push(message(colour, (2, s, t + 1), 0))
                push(mate_copy(q, i + 1, holder(axes, sign, s, t + 1)))
        if i == 0:
            for cp in norm_in:
                cp.wait_recv()
            total = nb_p[0]
            for o in range(1, n_pp):
                total = total + nb_p[o]
            norm_out, norm_in = norm_swap(total, nb_y, ny_s, ny_r, "dp", y, n_dp)
            for cp in norm_out:
                push(cp)
        if i == 1:
            for cp in norm_in:
                cp.wait_recv()
            total = nb_y[0]
            for o in range(1, n_dp):
                total = total + nb_y[o]
            norm_out, norm_in = norm_swap(total, nb_z, nz_s, nz_r, "tp", z, n_tp)
            for cp in norm_out:
                push(cp)
        if i == 2:
            for cp in norm_in:
                cp.wait_recv()
            total = nb_z[0]
            for o in range(1, n_tp):
                total = total + nb_z[o]
            norm = jnp.sqrt(jnp.sum(total, axis=(0, 1), keepdims=True))
            scale_ref[...] = jnp.broadcast_to(CLIP_NORM / jnp.maximum(norm, CLIP_NORM), (8, 128))

    for q, axes, sign, sizes, dest, plan in colours:
        for i in range(steps + 1):
            if i == 0:
                b = own
            else:
                phase, s, t = plan[i - 1]
                b = holder(axes, sign, s + 1, 0) if phase == 1 else holder(axes, sign, s, t + 1)
            mate_copy(q, i, b + 1 - 2 * c).wait_recv()
    for cp in (rel_a, rel_b, one_a, one_b, com_a, com_b, *sends):
        cp.wait_send()


def plane_gradient(table, hid, dx, labels, lookup, n_tp, n_dp, n_pp, vocab):
    _, rows, dim = table.shape
    tok = hid.shape[0]
    dq = dim // 4
    steps = (n_pp // 2) * n_dp
    full = pl.BlockSpec(memory_space=VMEM)
    half = VMEM((2, 2, rows, dq), F32)
    return pl.pallas_call(
        functools.partial(grad_kernel, n_tp, n_dp, n_pp, vocab),
        out_shape=(VMEM((n_dp * n_pp, 4, rows, dq), F32), jax.ShapeDtypeStruct((8, 128), F32)),
        in_specs=[full] * 5,
        out_specs=(full, full),
        scratch_shapes=[
            VMEM((n_dp, rows, tok), F32), VMEM((rows, tok), BF16), VMEM((n_dp, 4, rows, dq), F32),
            VMEM((2, tok), F32), VMEM((2, tok), F32), VMEM((n_pp - 1, 2, tok), F32), VMEM((n_tp - 1, 2, tok), F32),
            half, half, half,
            VMEM((n_pp, 8, 128), F32), VMEM((n_dp, 8, 128), F32), VMEM((n_tp, 8, 128), F32),
            DMA((n_pp - 1,)), DMA((n_pp - 1,)), DMA((n_tp - 1,)), DMA((n_tp - 1,)), DMA((6,)), DMA((6,)),
            DMA((n_pp - 1,)), DMA((n_pp - 1,)), DMA((n_dp - 1,)), DMA((n_dp - 1,)), DMA((n_tp - 1,)), DMA((n_tp - 1,)),
            DMA((4, steps)), DMA((4, steps)), DMA((4, steps)), DMA((4, steps)),
        ],
        compiler_params=pltpu.CompilerParams(collective_id=1, has_side_effects=True, vmem_limit_bytes=22 << 20),
        name="plane_gradient",
    )(in_vmem(table), in_vmem(hid), in_vmem(dx), labels, lookup)


def adamw_kernel(scale_ref, g_ref, e_ref, m_ref, v_ref, ne_ref, nm_ref, nv_ref, nb_ref):
    i = pl.program_id(0)
    dq = g_ref.shape[3]
    scale = scale_ref[0:1, 0:1]
    for q in range(4):
        cols = pl.ds(q * dq, dq)
        g = g_ref[i, q] * scale
        e = e_ref[:, cols]
        m = BETA_ONE * m_ref[:, cols] + (1.0 - BETA_ONE) * g
        v = BETA_TWO * v_ref[:, cols] + (1.0 - BETA_TWO) * g * g
        step = (m * (1.0 / (1.0 - BETA_ONE ** OPT_STEP))) / (jnp.sqrt(v * (1.0 / (1.0 - BETA_TWO ** OPT_STEP))) + ADAM_EPS)
        ne = e - LEARN_RATE * (step + WEIGHT_DECAY * e)
        ne_ref[:, cols] = ne
        nm_ref[:, cols] = m
        nv_ref[:, cols] = v
        nb_ref[:, cols] = ne.astype(BF16)


def adamw(scale, grad, master, exp_avg, exp_avg_sq):
    vocab, dim = master.shape
    tile = grad.shape[2]
    spec = pl.BlockSpec((tile, dim), lambda i: (i, 0))
    full = pl.BlockSpec(memory_space=VMEM)
    f32 = jax.ShapeDtypeStruct((vocab, dim), F32)
    count = vocab * dim
    return pl.pallas_call(
        adamw_kernel,
        out_shape=(f32, f32, f32, jax.ShapeDtypeStruct((vocab, dim), BF16)),
        grid=(grad.shape[0],),
        in_specs=[full, full, spec, spec, spec],
        out_specs=(spec,) * 4,
        cost_estimate=pl.CostEstimate(flops=20 * count, bytes_accessed=30 * count, transcendentals=2 * count),
        compiler_params=pltpu.CompilerParams(vmem_limit_bytes=32 << 20),
        name="adamw",
    )(scale, in_vmem(grad), master, exp_avg, exp_avg_sq)


def own_rows(master, n_dp, n_pp, rows):
    vocab, dim = master.shape
    p = lax.axis_index("pp")
    blocks = []
    for d in range(n_dp):
        first = (d * n_pp + p) * rows
        short = max(0, (d + 1) * n_pp * rows - vocab)
        start = jnp.minimum(first, vocab - rows)
        blk = lax.dynamic_slice_in_dim(master, start, rows, 0).astype(BF16)
        if short:
            blk = jnp.concatenate([blk, jnp.zeros((short, dim), BF16)], 0)
            blk = lax.dynamic_slice_in_dim(blk, first - start, rows, 0)
        blocks.append(blk)
    return jnp.stack(blocks)


def solution(mesh):
    n_pp, n_dp, n_tp = mesh.shape["pp"], mesh.shape["dp"], mesh.shape["tp"]
    table_spec = P("tp", None)

    def device_step(master, exp_avg, exp_avg_sq, stage_ids, stage_acts):
        vocab, dim = master.shape
        tok = stage_ids.shape[1] * stage_ids.shape[2]
        rows = -(-vocab // (n_pp * n_dp))
        rows = -(-rows // 8) * 8
        acts = stage_acts.reshape(tok, dim).astype(F32)
        hid, dx, labels, lookup = spread(acts, stage_ids.reshape(1, tok), n_tp, n_pp)
        table = own_rows(master, n_dp, n_pp, rows)
        grad, scale = plane_gradient(table, hid, dx, labels, lookup, n_tp, n_dp, n_pp, vocab)
        return adamw(scale, grad, master, exp_avg, exp_avg_sq)

    return jax.shard_map(device_step, mesh=mesh, in_specs=(table_spec, table_spec, table_spec, P("pp", "dp", None), P("pp", "dp", None, None)), out_specs=(table_spec, table_spec, table_spec, table_spec), check_vma=False)
```

time: 948 us -> 282 us (0.30)
  waiting for transfers between devices: 726 us -> 0 us
  Pallas kernels: 0 us -> 272 us
  other arithmetic: 94.2 us -> 1.15 us
  matrix products: 65.1 us -> 0 us
  blocking collectives: 43.2 us -> 0 us
  between operations: 14.9 us -> 0.74 us
    psum x2 -> x0, waiting for transfers between devices: 726 us -> none  [the longest x1 447 us: device_step(): gradient = lax.psum(stage_sum, 'dp') / n_repl]
    pallas_call x0 -> x3, Pallas kernels: none -> 272 us  [the longest x1 133 us: plane_gradient(): pl.pallas_call(functools.partial(grad_kernel, n_tp, n_dp, n_pp, vocab), o...]
    dot_general x2 -> x0, matrix products: 65.1 us -> none  [the longest x1 34.6 us: stage_grad(): jnp.einsum('tv,td->vd', coeff_mat, act_flat, preferred_element_type=jnp.f...]
    convert_element_type x1, other arithmetic: 66 us -> 0.94 us  [device_step(): acts = stage_acts.reshape(tok, dim).astype(F32)]
    reduce_sum x2 -> x0, other arithmetic: 27.4 us -> none  [the longest x1 15.1 us: stage_grad(): row_sum = lax.psum(jnp.sum(exp_logits, axis=1), 'tp')]
    psum x2 -> x0, blocking collectives: 25.7 us -> none  [the longest x1 14.5 us: adamw_update(): sq_total = lax.psum(jnp.sum(gradient * gradient), 'tp')]
    pmax x1 -> x0, blocking collectives: 17.5 us -> none  [stage_grad(): row_max = lax.pmax(jnp.max(logits, axis=1), 'tp')]
  transfers between devices with their start and end apart: 2 -> 0, of which waited for: 2 -> 0; matrix products, arithmetic and copies ran while one was open for 0% -> 0% of each run, Pallas kernels for 0% -> 0%
where the time goes in v2:
time: 282 us; the launch traced here: 281 us
  Pallas kernels  272 us (96%)
  local copies, waits for them, and re-layouts  7.43 us (3%)
    pallas_call x1, Pallas kernels, plane_gradient(): pl.pallas_call(functools.partial(grad_kernel, n_tp, n_dp, n_pp, vocab), o...  133 us
    pallas_call x1, Pallas kernels, adamw(): pl.pallas_call(adamw_kernel, out_shape=(f32, f32, f32, jax.ShapeDtypeStru...  76.4 us
    pallas_call x1, Pallas kernels, spread(): pl.pallas_call(functools.partial(spread_kernel, n_tp, n_pp, n_chunk), out...  62.6 us

profile of v2, /device:TPU:1, one launch (start us, length us, event | category | flops | bytes accessed | tf_op | source)
XLA Modules:
  0.0 281.4 jit_solution(18217559788858395018)
XLA Ops:
  0.6 0.0 copy-start.5
  0.7 2.6 fusion.1
  3.2 0.1 fusion
  3.4 0.2 pad_maximum_fusion.tab_ref
  3.6 0.0 copy-done.5
  3.6 0.0 copy-start.2
  3.6 0.9 bitcast_convert_fusion.acts_ref
  4.5 0.0 copy-done.2
  4.6 62.6 %spread.1 = (bf16[1536,1024]{1,0:T(8,128)(2,1)S(1)}, bf16[1536,1024]{1,0:T(8,128)(2,1)S(1)}, s32[1,1536]{1,0:T(1,128)S(1)}, s32[1,1536]{1,0:T(1,128)S(1)}) custom-call(f32[1536,1024]{1,0:T(8,128)S(1)} %bitcast_convert_fusion.acts_ref, s32[1,1536]{1,0:T(1,128)S(1)} %bitcast.12), custom_call_target="tpu_custom_call" | custom-call | tf_op jit(solution)/shard_map/spread/pallas_call | solution.py:183
  67.1 0.0 copy-start
  67.1 1.7 copy-done
  68.8 0.0 copy-start.3
  68.8 0.6 copy-done.3
  69.4 0.0 copy-start.4
  69.4 0.6 copy-done.4
  70.0 0.0 copy-start.1
  70.0 1.9 copy-done.1
  71.9 133.1 %plane_gradient.1 = (f32[32,4,200,256]{3,2,1,0:T(8,128)S(1)}, f32[8,128]{1,0:T(8,128)}) custom-call(bf16[4,200,1024]{2,1,0:T(8,128)(2,1)S(1)} %pad_maximum_fusion.tab_ref, bf16[1536,1024]{1,0:T(8,128)(2,1)S(1)} %get-tuple-element.10.hid_ref, bf16[1536,1024]{1,0:T(8,128)(2,1)S(1)} %copy-done.1, s32[1,1536]{1,0:T(1,128)} %copy-done.3, s32[1,1536]{1,0:T(1,128)} %copy-done.4), custom_call_target="tpu_custom_call" | custom-call | tf_op jit(solution)/shard_map/plane_gradient/pallas_call | solution.py:430
  205.0 76.4 %adamw.1 = (f32[6288,1024]{1,0:T(8,128)}, f32[6288,1024]{1,0:T(8,128)}, f32[6288,1024]{1,0:T(8,128)}, bf16[6288,1024]{1,0:T(8,128)(2,1)}) custom-call(f32[8,128]{1,0:T(8,128)} %get-tuple-element.14.scale_ref, f32[32,4,200,256]{3,2,1,0:T(8,128)S(1)} %get-tuple-element.15.g_ref, f32[6288,1024]{1,0:T(8,128)} %e_ref.1, f32[6288,1024]{1,0:T(8,128)} %m_ref.1, ...), custom_call_target="tpu_custom_call" | custom-call | flops 128778240 | bytes 193167360 | tf_op jit(solution)/shard_map/adamw/pallas_call | solution.py:474
Async XLA Ops:
  0.6 2.9 %copy-start.5 = (bf16[1,6,256,1024]{3,2,1,0:T(8,128)(2,1)S(1)}, bf16[1,6,256,1024]{3,2,1,0:T(8,128)(2,1)}, u32[]{:S(2)}) copy-start(bf16[1,6,256,1024]{3,2,1,0:T(8,128)(2,1)} %param.9) | copy-start | bytes 9437188
  3.6 1.0 copy-start.2
  67.1 1.7 copy-start
  68.8 0.6 copy-start.3
  69.4 0.6 copy-start.4
  70.0 1.9 copy-start.1

commit v3 on v2

v3 whole, which is shorter than its diff:
```python
import functools

import jax
import jax.numpy as jnp
from jax import lax
from jax.experimental import pallas as pl
from jax.experimental.pallas import tpu as pltpu
from jax.sharding import PartitionSpec as P

LEARN_RATE = 0.003
BETA_ONE = 0.9
BETA_TWO = 0.95
ADAM_EPS = 1e-8
WEIGHT_DECAY = 0.1
CLIP_NORM = 1.0
OPT_STEP = 10

MESH_ID = pl.DeviceIdType.MESH
LOW = -1e30
VMEM = pltpu.VMEM
DMA = pltpu.SemaphoreType.DMA
F32, BF16 = jnp.float32, jnp.bfloat16


def remote(src, dst, send, recv, where):
    return pltpu.make_async_remote_copy(src_ref=src, dst_ref=dst, send_sem=send, recv_sem=recv, device_id=where, device_id_type=MESH_ID)


def in_vmem(arr):
    return pltpu.with_memory_space_constraint(arr, VMEM)


def enter(groups):
    barrier = pltpu.get_barrier_semaphore()
    for axis, peer in groups:
        pl.semaphore_signal(barrier, inc=1, device_id={axis: peer}, device_id_type=MESH_ID)
    pl.semaphore_wait(barrier, len(groups))


def ring_plan(n_one, n_two):
    items = [(1, s, 0) for s in range(n_one - 1)] + [(2, s, t) for s in range(n_one) for t in range(n_two - 1)]
    return sorted(items, key=lambda i: (i[1] + i[2], i[0], i[2]))


def grad_kernel(n_tp, n_dp, n_pp, n_chunk, table_ref, acts_ref, ids_ref, g_ref, scale_ref, hid_buf, dx_buf, hid_ref, dx_ref, lab_ref, look_ref, tab_ref, exp_ref, dl_ref, part_ref, stat_ref, mid_ref, buf_p, buf_z, rel_ref, one_ref, com_ref, nb_p, nb_y, nb_z, load_s, feed_s, send_x, send_z, send_d, send_e, recv_x, recv_z, recv_d, recv_e, id_s, id_r, sp_s, sp_r, sz_s, sz_r, rs_s, rs_r, np_s, np_r, ny_s, ny_r, nz_s, nz_r, ag_s, ag_r, d_s, d_r):
    p, z, y = lax.axis_index("pp"), lax.axis_index("tp"), lax.axis_index("dp")
    n_x = n_pp // 2
    x, c, par = p // 2, lax.rem(p, 2), lax.rem(z, 2)
    mate = 2 * x + 1 - c
    vocab = table_ref.shape[0]
    rows, tok = exp_ref.shape[1:]
    dq = g_ref.shape[3]
    up_y, down_y = lax.rem(y + 1, n_dp), lax.rem(y + n_dp - 1, n_dp)

    def first_row(d):
        return (d * n_pp + p) * rows

    short = vocab - (n_dp * n_pp - 1) * rows

    def table_copies(count, blocks):
        return [pltpu.make_async_copy(table_ref.at[pl.ds(pl.multiple_of(first_row(d), 8), count), pl.ds(q * dq, dq)], part_ref.at[d, q, pl.ds(0, count)], load_s.at[1 + 4 * d + q]) for d in blocks for q in range(4)]

    def each_table_copy(act):
        for cp in table_copies(rows, range(n_dp - 1)):
            act(cp)
        for cond, count in ((p < n_pp - 1, rows), (p == n_pp - 1, short)):
            @pl.when(cond)
            def _(count=count):
                for cp in table_copies(count, (n_dp - 1,)):
                    act(cp)

    each_table_copy(lambda cp: cp.start())
    sources = ((n_pp - 1, hid_buf, hid_ref, lab_ref), (0, dx_buf, dx_ref, look_ref))
    for source, _, low, _ in sources:
        @pl.when(p == source)
        def _(low=low):
            pltpu.make_async_copy(acts_ref, low, load_s.at[0]).start()

    enter([("pp", lax.rem(p + o, n_pp)) for o in range(1, n_pp)] + [("tp", lax.rem(z + o, n_tp)) for o in range(1, n_tp)] + [("dp", lax.rem(y + o, n_dp)) for o in range(1, n_dp)])

    step_x = 1 - 2 * c
    next_p = 2 * lax.rem(x + step_x + n_x, n_x) + c
    next_z = lax.rem(z + step_x + n_tp, n_tp)
    size = tok // (4 * n_chunk)
    lag = 2

    def span(core, parity, k):
        return pl.ds(pl.multiple_of(((2 * parity + core) * n_chunk + k) * size, 8), size)

    class Stream:
        def __init__(self, a):
            self.a = a
            self.source, self.buf, self.low, self.ids = sources[a]
            self.is_src = p == self.source
            s_x = self.source // 2
            self.dist = lax.rem(jnp.where(c == 0, x - s_x, s_x - x) + n_x, n_x)

        def hop(self, part, send, recv, where):
            return remote(self.buf.at[part], self.buf.at[part], send, recv, where)

        def feed(self, k):
            return self.hop(span(1 - c, par, k), feed_s.at[self.a, k], recv_x.at[self.a, k], {"pp": mate})

        def ring(self, k):
            return self.hop(span(c, par, k), send_x.at[self.a, k], recv_x.at[self.a, k], {"pp": next_p})

        def plane(self, k, parity):
            return self.hop(span(c, parity, k), send_z.at[self.a, k], recv_z.at[self.a, k], {"tp": next_z})

        def across(self, k, core):
            return self.hop(span(core, par, k), send_d.at[self.a, k], recv_d.at[self.a, k], {"pp": mate})

        def again(self, k, core):
            return self.hop(span(core, 1 - par, k), send_e.at[self.a, k], recv_e.at[self.a, k], {"pp": mate})

        def id_copy(self, o):
            return remote(ids_ref, self.ids, id_s.at[self.a, o - 1], id_r.at[self.a], {"pp": lax.rem(p + o, n_pp)})

        def begin(self):
            @pl.when(self.is_src)
            def _():
                pltpu.make_async_copy(acts_ref, self.low, load_s.at[0]).wait()
                self.ids[...] = ids_ref[...]

                @pl.loop(0, n_chunk)
                def _(k):
                    def widen(part):
                        self.buf[part, :] = self.low[part, :].astype(F32)

                    widen(span(1 - c, par, k))
                    self.feed(k).start()
                    widen(span(c, par, k))
                    if n_x > 1:
                        self.ring(k).start()
                    self.across(k, c).start()
                    widen(span(c, 1 - par, k))
                    self.again(k, c).start()

                for o in range(1, n_pp):
                    self.id_copy(o).start()

        def steps(self, lo, hi):
            @pl.when(jnp.logical_not(self.is_src))
            def _():
                @pl.loop(lo, hi)
                def _(k):
                    @pl.when(k < n_chunk)
                    def _():
                        self.ring(k).wait_recv()
                        if n_x > 1:
                            @pl.when(self.dist < n_x - 1)
                            def _():
                                self.ring(k).start()

                        self.plane(k, par).start()

                        @pl.when(mate != self.source)
                        def _():
                            self.across(k, c).start()

                    @pl.when(k >= lag)
                    def _():
                        self.plane(k - lag, 1 - par).wait_recv()

                        @pl.when(mate != self.source)
                        def _():
                            self.again(k - lag, c).start()

        def collect(self):
            @pl.when(jnp.logical_not(self.is_src))
            def _():
                self.id_copy(1).wait_recv()

                @pl.loop(0, n_chunk)
                def _(k):
                    self.across(k, 1 - c).wait_recv()
                    self.again(k, 1 - c).wait_recv()

                tile = min(128, tok)

                @pl.loop(0, tok // tile)
                def _(k):
                    here = pl.ds(pl.multiple_of(k * tile, tile), tile)
                    self.low[here, :] = self.buf[here, :].astype(BF16)

        def settle(self):
            @pl.when(self.is_src)
            def _():
                for o in range(1, n_pp):
                    self.id_copy(o).wait_send()

            @pl.loop(0, n_chunk)
            def _(k):
                @pl.when(self.is_src)
                def _():
                    self.feed(k).wait_send()

                @pl.when(jnp.logical_not(self.is_src))
                def _():
                    self.plane(k, par).wait_send()

                if n_x > 1:
                    @pl.when(self.dist < n_x - 1)
                    def _():
                        self.ring(k).wait_send()

                @pl.when(mate != self.source)
                def _():
                    self.across(k, c).wait_send()
                    self.again(k, c).wait_send()

    hid_in, dx_in = Stream(0), Stream(1)
    hid_in.begin()
    each_table_copy(lambda cp: cp.wait())
    for d in range(n_dp):
        for q in range(4):
            tab_ref[d, :, q * dq:(q + 1) * dq] = part_ref[d, q].astype(BF16)
    hid_in.steps(0, n_chunk + lag)
    dx_in.begin()
    hid_in.collect()

    wide = min(256, tok)

    @pl.loop(0, tok // wide)
    def _(j):
        cols = pl.ds(pl.multiple_of(j * wide, wide), wide)
        h = hid_ref[cols, :]
        top = jnp.full((1, wide), LOW, F32)
        for d in range(n_dp):
            lg = lax.dot_general(tab_ref[d], h, (((1,), (1,)), ((), ())), preferred_element_type=F32)
            if d == n_dp - 1 and short < rows:
                ok = first_row(d) + lax.broadcasted_iota(jnp.int32, (rows, wide), 0) < vocab
                lg = jnp.where(ok, lg, LOW)
            exp_ref[d, :, cols] = lg
            top = jnp.maximum(top, jnp.max(lg, axis=0, keepdims=True))
        tot = jnp.zeros((1, wide), F32)
        for d in range(n_dp):
            e = jnp.exp(exp_ref[d, :, cols] - top)
            exp_ref[d, :, cols] = e
            tot = tot + jnp.sum(e, axis=0, keepdims=True)
        stat_ref[0:1, cols] = top
        stat_ref[1:2, cols] = tot

    def swap(src, buf, send, recv, axis, me, n):
        return [remote(src, buf.at[o - 1], send.at[o - 1], recv.at[o - 1], {axis: lax.rem(me + o, n)}) for o in range(1, n)]

    def merge(src, buf, n):
        top = src[0:1, :]
        for o in range(1, n):
            top = jnp.maximum(top, buf[o - 1, 0:1, :])
        tot = src[1:2, :] * jnp.exp(src[0:1, :] - top)
        for o in range(1, n):
            tot = tot + buf[o - 1, 1:2, :] * jnp.exp(buf[o - 1, 0:1, :] - top)
        return top, tot

    def local_ids(ref):
        ids = ref[...] - z * vocab
        return jnp.where(ids < vocab, ids, -1)

    def row_ids(d):
        return first_row(d) + lax.broadcasted_iota(jnp.int32, (rows, tok), 0)

    third = (n_chunk + lag) // 3
    stage = swap(stat_ref, buf_p, sp_s, sp_r, "pp", p, n_pp)
    for cp in stage:
        cp.start()
    dx_in.steps(0, third)
    for cp in stage:
        cp.wait()
    top, tot = merge(stat_ref, buf_p, n_pp)
    mid_ref[0:1, :] = top
    mid_ref[1:2, :] = tot
    stage = swap(mid_ref, buf_z, sz_s, sz_r, "tp", z, n_tp)
    for cp in stage:
        cp.start()
    dx_in.steps(third, 2 * third)
    for cp in stage:
        cp.wait()
    top, tot = merge(mid_ref, buf_z, n_tp)
    mid_ref[0:1, :] = jnp.exp(stat_ref[0:1, :] - top) / (tot * tok)

    def head(d):
        prob = exp_ref[d] * mid_ref[0:1, :]
        hit = local_ids(lab_ref) == row_ids(d)
        dl_ref[...] = jnp.where(hit, prob - 1.0 / tok, prob).astype(BF16)
        for q in range(4):
            part_ref[d, q] = jnp.dot(dl_ref[...], hid_ref[:, q * dq:(q + 1) * dq], preferred_element_type=F32)

    def lookup(d):
        dl_ref[...] = (local_ids(look_ref) == row_ids(d)).astype(BF16)
        for q in range(4):
            part_ref[d, q] += jnp.dot(dl_ref[...], dx_ref[:, q * dq:(q + 1) * dq], preferred_element_type=F32)

    pl.loop(0, n_dp)(head)
    dx_in.steps(2 * third, n_chunk + lag)
    dx_in.collect()

    lo, hi = pl.ds(0, 2), pl.ds(2, 2)
    far = lax.rem(y + 2, n_dp)
    rel_a = remote(part_ref.at[far, lo], rel_ref.at[0], rs_s.at[0], rs_r.at[0], {"dp": up_y})
    rel_b = remote(part_ref.at[far, hi], rel_ref.at[1], rs_s.at[1], rs_r.at[1], {"dp": down_y})
    one_b = remote(part_ref.at[up_y, hi], one_ref.at[1], rs_s.at[2], rs_r.at[2], {"dp": up_y})
    one_a = remote(part_ref.at[down_y, lo], one_ref.at[0], rs_s.at[3], rs_r.at[3], {"dp": down_y})
    com_a = remote(part_ref.at[up_y, lo], com_ref.at[0], rs_s.at[4], rs_r.at[4], {"dp": up_y})
    com_b = remote(part_ref.at[down_y, hi], com_ref.at[1], rs_s.at[5], rs_r.at[5], {"dp": down_y})
    lookup(far)
    rel_a.start()
    rel_b.start()
    lookup(up_y)
    one_b.start()
    lookup(down_y)
    one_a.start()
    lookup(y)
    rel_a.wait_recv()
    part_ref[up_y, lo] += rel_ref[0]
    com_a.start()
    rel_b.wait_recv()
    part_ref[down_y, hi] += rel_ref[1]
    com_b.start()
    own = y * n_pp + p
    square = jnp.zeros((8, 128), F32)
    one_a.wait_recv()
    one_b.wait_recv()
    for half, cp in ((0, com_a), (1, com_b)):
        cp.wait_recv()
        for q in range(2):
            total = (part_ref[y, 2 * half + q] + com_ref[half, q] + one_ref[half, q]) * (1.0 / n_dp)
            g_ref[own, 2 * half + q] = total
            lanes = jnp.sum((total * total).reshape(rows // 8, 8, dq), axis=0)
            for i in range(0, dq, 128):
                square = square + lanes[:, i:i + 128]

    def block(xx, yy):
        return lax.rem(yy + 2 * n_dp, n_dp) * n_pp + 2 * lax.rem(xx + 2 * n_x, n_x) + c

    colours = []
    for q, (axes, sign) in enumerate((("xy", 1), ("xy", -1), ("yx", 1), ("yx", -1))):
        sizes = (n_x, n_dp) if axes == "xy" else (n_dp, n_x)
        to_x = {"pp": 2 * lax.rem(x + sign + n_x, n_x) + c}
        to_y = {"dp": lax.rem(y + sign + n_dp, n_dp)}
        dest = (to_x, to_y) if axes == "xy" else (to_y, to_x)
        colours.append((q, axes, sign, sizes, dest, ring_plan(*sizes)))

    def holder(axes, sign, s, t):
        return block(x - sign * s, y - sign * t) if axes == "xy" else block(x - sign * t, y - sign * s)

    def message(colour, item, coming):
        q, axes, sign, _, dest, plan = colour
        phase, s, t = item
        at = plan.index(item)
        s_at, t_at = (s + coming, t) if phase == 1 else (s, t + coming)
        b = holder(axes, sign, s_at, t_at)
        return remote(g_ref.at[b, q], g_ref.at[b, q], ag_s.at[q, at], ag_r.at[q, at], dest[phase - 1])

    def mate_copy(q, slot, b):
        return remote(g_ref.at[b, q], g_ref.at[b, q], d_s.at[q, slot], d_r.at[q, slot], {"pp": mate})

    sends = []

    def push(cp):
        cp.start()
        sends.append(cp)

    for colour in colours:
        if colour[3][0] > 1:
            push(message(colour, (1, 0, 0), 0))
    for colour in colours:
        if colour[3][1] > 1:
            push(message(colour, (2, 0, 0), 0))

    def norm_swap(value, buf, send, recv, axis, me, n):
        buf[me] = value
        return [remote(buf.at[me], buf.at[me], send.at[o - 1], recv.at[o - 1], {axis: lax.rem(me + o, n)}) for o in range(1, n)], [
            remote(buf.at[lax.rem(me + n - o, n)], buf.at[lax.rem(me + n - o, n)], send.at[o - 1], recv.at[o - 1], {axis: lax.rem(me + o, n)}) for o in range(1, n)]

    norm_out, norm_in = norm_swap(square, nb_p, np_s, np_r, "pp", p, n_pp)
    for cp in norm_out:
        push(cp)
    for q in range(4):
        push(mate_copy(q, 0, own))

    steps = n_x * n_dp - 1
    for i in range(steps):
        for colour in colours:
            q, axes, sign, sizes, dest, plan = colour
            phase, s, t = plan[i]
            message(colour, plan[i], 1).wait_recv()
            if phase == 1:
                if s + 1 < sizes[0] - 1:
                    push(message(colour, (1, s + 1, 0), 0))
                if sizes[1] > 1:
                    push(message(colour, (2, s + 1, 0), 0))
                push(mate_copy(q, i + 1, holder(axes, sign, s + 1, 0)))
            else:
                if t + 1 < sizes[1] - 1:
                    push(message(colour, (2, s, t + 1), 0))
                push(mate_copy(q, i + 1, holder(axes, sign, s, t + 1)))
        if i == 0:
            for cp in norm_in:
                cp.wait_recv()
            total = nb_p[0]
            for o in range(1, n_pp):
                total = total + nb_p[o]
            norm_out, norm_in = norm_swap(total, nb_y, ny_s, ny_r, "dp", y, n_dp)
            for cp in norm_out:
                push(cp)
        if i == 1:
            for cp in norm_in:
                cp.wait_recv()
            total = nb_y[0]
            for o in range(1, n_dp):
                total = total + nb_y[o]
            norm_out, norm_in = norm_swap(total, nb_z, nz_s, nz_r, "tp", z, n_tp)
            for cp in norm_out:
                push(cp)
        if i == 2:
            for cp in norm_in:
                cp.wait_recv()
            total = nb_z[0]
            for o in range(1, n_tp):
                total = total + nb_z[o]
            norm = jnp.sqrt(jnp.sum(total, axis=(0, 1), keepdims=True))
            scale_ref[...] = jnp.broadcast_to(CLIP_NORM / jnp.maximum(norm, CLIP_NORM), (8, 128))

    for q, axes, sign, sizes, dest, plan in colours:
        for i in range(steps + 1):
            if i == 0:
                b = own
            else:
                phase, s, t = plan[i - 1]
                b = holder(axes, sign, s + 1, 0) if phase == 1 else holder(axes, sign, s, t + 1)
            mate_copy(q, i, b + 1 - 2 * c).wait_recv()
    for cp in (rel_a, rel_b, one_a, one_b, com_a, com_b, *sends):
        cp.wait_send()
    hid_in.settle()
    dx_in.settle()


def plane_gradient(master, acts, ids, n_tp, n_dp, n_pp):
    vocab, dim = master.shape
    tok = acts.shape[0]
    rows = -(-vocab // (n_pp * n_dp))
    rows = -(-rows // 8) * 8
    dq = dim // 4
    n_chunk = 12 if tok % (4 * 12 * 8) == 0 else 2
    steps = (n_pp // 2) * n_dp
    full = pl.BlockSpec(memory_space=VMEM)
    any_space = pl.BlockSpec(memory_space=pl.ANY)
    half = VMEM((2, 2, rows, dq), F32)
    chunk = DMA((2, n_chunk))
    return pl.pallas_call(
        functools.partial(grad_kernel, n_tp, n_dp, n_pp, n_chunk),
        out_shape=(VMEM((n_dp * n_pp, 4, rows, dq), F32), jax.ShapeDtypeStruct((8, 128), F32)),
        in_specs=[any_space, any_space, full],
        out_specs=(full, full),
        scratch_shapes=[
            VMEM((tok, dim), F32), VMEM((tok, dim), F32), VMEM((tok, dim), BF16), VMEM((tok, dim), BF16),
            VMEM((1, tok), jnp.int32), VMEM((1, tok), jnp.int32), VMEM((n_dp, rows, dim), BF16),
            VMEM((n_dp, rows, tok), F32), VMEM((rows, tok), BF16), VMEM((n_dp, 4, rows, dq), F32),
            VMEM((2, tok), F32), VMEM((2, tok), F32), VMEM((n_pp - 1, 2, tok), F32), VMEM((n_tp - 1, 2, tok), F32),
            half, half, half,
            VMEM((n_pp, 8, 128), F32), VMEM((n_dp, 8, 128), F32), VMEM((n_tp, 8, 128), F32),
            DMA((1 + 4 * n_dp,)), *[chunk] * 9, DMA((2, n_pp - 1)), DMA((2,)),
            DMA((n_pp - 1,)), DMA((n_pp - 1,)), DMA((n_tp - 1,)), DMA((n_tp - 1,)), DMA((6,)), DMA((6,)),
            DMA((n_pp - 1,)), DMA((n_pp - 1,)), DMA((n_dp - 1,)), DMA((n_dp - 1,)), DMA((n_tp - 1,)), DMA((n_tp - 1,)),
            DMA((4, steps)), DMA((4, steps)), DMA((4, steps)), DMA((4, steps)),
        ],
        compiler_params=pltpu.CompilerParams(collective_id=0, has_side_effects=True, vmem_limit_bytes=34 << 20),
        name="plane_gradient",
    )(master, acts, ids)


def adamw_kernel(n_slot, ahead, scale_ref, g_ref, e_hbm, m_hbm, v_hbm, ne_hbm, nm_hbm, nv_hbm, nb_hbm, e_buf, m_buf, v_buf, b_buf, in_s, out_s):
    n_blk, _, rows, dq = g_ref.shape
    vocab = e_hbm.shape[0]
    last = vocab - (n_blk - 1) * rows
    scale = scale_ref[0:1, 0:1]

    def loads(i, count):
        slot = lax.rem(i, n_slot)
        here = pl.ds(pl.multiple_of(i * rows, 8), count)
        return [pltpu.make_async_copy(hbm.at[here], buf.at[slot, pl.ds(0, count)], in_s.at[a, slot]) for a, (hbm, buf) in enumerate(((e_hbm, e_buf), (m_hbm, m_buf), (v_hbm, v_buf)))]

    def stores(i, count):
        slot = lax.rem(i, n_slot)
        here = pl.ds(pl.multiple_of(i * rows, 8), count)
        return [pltpu.make_async_copy(buf.at[slot, pl.ds(0, count)], hbm.at[here], out_s.at[a, slot]) for a, (buf, hbm) in enumerate(((e_buf, ne_hbm), (m_buf, nm_hbm), (v_buf, nv_hbm), (b_buf, nb_hbm)))]

    def each(copies, i, act):
        if last == rows:
            for cp in copies(i, rows):
                act(cp)
            return
        for cond, count in ((i < n_blk - 1, rows), (i == n_blk - 1, last)):
            @pl.when(cond)
            def _(count=count):
                for cp in copies(i, count):
                    act(cp)

    for i in range(min(ahead, n_blk)):
        each(loads, i, lambda cp: cp.start())

    @pl.loop(0, n_blk)
    def _(i):
        slot = lax.rem(i, n_slot)

        @pl.when(i + ahead < n_blk)
        def _():
            @pl.when(i + ahead >= n_slot)
            def _():
                each(stores, i + ahead - n_slot, lambda cp: cp.wait())

            each(loads, i + ahead, lambda cp: cp.start())

        each(loads, i, lambda cp: cp.wait())

        @pl.loop(0, rows // 8, unroll=5 if rows % 40 == 0 else 1)
        def _(r):
            at = pl.ds(pl.multiple_of(r * 8, 8), 8)
            for q in range(4):
                cols = pl.ds(q * dq, dq)
                g = g_ref[i, q, at, :] * scale
                e = e_buf[slot, at, cols]
                m = BETA_ONE * m_buf[slot, at, cols] + (1.0 - BETA_ONE) * g
                v = BETA_TWO * v_buf[slot, at, cols] + (1.0 - BETA_TWO) * g * g
                step = (m * (1.0 / (1.0 - BETA_ONE ** OPT_STEP))) / (jnp.sqrt(v * (1.0 / (1.0 - BETA_TWO ** OPT_STEP))) + ADAM_EPS)
                ne = e - LEARN_RATE * (step + WEIGHT_DECAY * e)
                e_buf[slot, at, cols] = ne
                m_buf[slot, at, cols] = m
                v_buf[slot, at, cols] = v
                b_buf[slot, at, cols] = ne.astype(BF16)

        each(stores, i, lambda cp: cp.start())

    for i in range(max(0, n_blk - n_slot), n_blk):
        each(stores, i, lambda cp: cp.wait())


def adamw(scale, grad, master, exp_avg, exp_avg_sq):
    vocab, dim = master.shape
    rows = grad.shape[2]
    n_slot = 6
    full = pl.BlockSpec(memory_space=VMEM)
    any_space = pl.BlockSpec(memory_space=pl.ANY)
    f32 = jax.ShapeDtypeStruct((vocab, dim), F32)
    count = vocab * dim
    ring = VMEM((n_slot, rows, dim), F32)
    return pl.pallas_call(
        functools.partial(adamw_kernel, n_slot, 3),
        out_shape=(f32, f32, f32, jax.ShapeDtypeStruct((vocab, dim), BF16)),
        in_specs=[full, full, any_space, any_space, any_space],
        out_specs=(any_space,) * 4,
        scratch_shapes=[ring, ring, ring, VMEM((n_slot, rows, dim), BF16), DMA((3, n_slot)), DMA((4, n_slot))],
        cost_estimate=pl.CostEstimate(flops=20 * count, bytes_accessed=30 * count, transcendentals=2 * count),
        compiler_params=pltpu.CompilerParams(vmem_limit_bytes=32 << 20),
        name="adamw",
    )(scale, in_vmem(grad), master, exp_avg, exp_avg_sq)


def solution(mesh):
    n_pp, n_dp, n_tp = mesh.shape["pp"], mesh.shape["dp"], mesh.shape["tp"]
    table_spec = P("tp", None)

    def device_step(master, exp_avg, exp_avg_sq, stage_ids, stage_acts):
        vocab, dim = master.shape
        tok = stage_ids.shape[1] * stage_ids.shape[2]
        acts = stage_acts.reshape(tok, dim)
        grad, scale = plane_gradient(master, acts, stage_ids.reshape(1, tok), n_tp, n_dp, n_pp)
        return adamw(scale, grad, master, exp_avg, exp_avg_sq)

    return jax.shard_map(device_step, mesh=mesh, in_specs=(table_spec, table_spec, table_spec, P("pp", "dp", None), P("pp", "dp", None, None)), out_specs=(table_spec, table_spec, table_spec, table_spec), check_vma=False)
```

time: 282 us -> 248 us (0.88)
  Pallas kernels: 272 us -> 247 us
  local copies, waits for them, and re-layouts: 7.43 us -> 0 us
    pallas_call x3 -> x2, Pallas kernels: 272 us -> 247 us  [the longest x1 191 us: plane_gradient(): pl.pallas_call(functools.partial(grad_kernel, n_tp, n_dp, n_pp, n_chunk),...]
    unnamed x12 -> x0, local copies, waits for them, and re-layouts: 4.74 us -> none
where the time goes in v3:
time: 248 us
  Pallas kernels  247 us (100%)
    pallas_call x1, Pallas kernels, plane_gradient(): pl.pallas_call(functools.partial(grad_kernel, n_tp, n_dp, n_pp, n_chunk),...  191 us
    pallas_call x1, Pallas kernels, adamw(): pl.pallas_call(functools.partial(adamw_kernel, n_slot, 3), out_shape=(f32...  56.5 us

profile of v3, /device:TPU:1, one launch (start us, length us, event | category | flops | bytes accessed | tf_op | source)
XLA Modules:
  0.0 248.1 jit_solution(15849787891064805398)
XLA Ops:
  0.6 191.0 %plane_gradient.1 = (f32[32,4,200,256]{3,2,1,0:T(8,128)S(1)}, f32[8,128]{1,0:T(8,128)}) custom-call(f32[6288,1024]{1,0:T(8,128)} %e_hbm.1, bf16[1536,1024]{1,0:T(8,128)(2,1)} %bitcast.2, s32[1,1536]{1,0:T(1,128)} %bitcast.3), custom_call_target="tpu_custom_call" | custom-call | tf_op jit(solution)/shard_map/plane_gradient/pallas_call | solution.py:451
  191.6 56.5 %adamw.1 = (f32[6288,1024]{1,0:T(8,128)}, f32[6288,1024]{1,0:T(8,128)}, f32[6288,1024]{1,0:T(8,128)}, bf16[6288,1024]{1,0:T(8,128)(2,1)}) custom-call(f32[8,128]{1,0:T(8,128)} %get-tuple-element.6.scale_ref, f32[32,4,200,256]{3,2,1,0:T(8,128)S(1)} %get-tuple-element.7.g_ref, f32[6288,1024]{1,0:T(8,128)} %e_hbm.1, f32[6288,1024]{1,0:T(8,128)} %m_hbm.1, ...), custom_call_target="tpu_custom_call" | custom-call | flops 128778240 | bytes 193167360 | tf_op jit(solution)/shard_map/adamw/pallas_call | solution.py:548
